TPU v7x, 32 devices: a whole 2x2x4 slice. The times are simulated.
32 devices in a mesh: seq: 8 (over z, x), head: 4 (over y, core).
Axes of the slice: x: 2, y: 2, z: 4, core: 2. Of those that a mesh axis runs over, the one named last changes fastest.
Arguments:
- context: bfloat16 [4, 4096, 1024], P('head', 'seq'), may hold values from -6 to 6
- latents: bfloat16 [4, 1024, 1024], P('head'), may hold values from -6 to 6
- offsets: int32 [4], P('head'), may hold values from 0 to 3072
- query_gain: float32 [1024], replicated, may hold values from 0.1 to 1.9
- key_gain: float32 [1024], replicated, may hold values from 0.1 to 1.9
- layer_gain: float32 [2, 1024], replicated, may hold values from 0.1 to 1.9
- cross_query: bfloat16 [1024, 1024], P(('seq', 'head')), may hold values from -0.25 to 0.25
- cross_key: bfloat16 [1024, 1024], P(('seq', 'head')), may hold values from -0.25 to 0.25
- cross_value: bfloat16 [1024, 1024], P(('seq', 'head')), may hold values from -0.1875 to 0.1875
- cross_out: bfloat16 [1024, 1024], P(('seq', 'head')), may hold values from -0.1875 to 0.1875
- layer_qkv: bfloat16 [2, 1024, 3072], P(None, ('seq', 'head')), may hold values from -0.25 to 0.25
- layer_out: bfloat16 [2, 1024, 1024], P(None, ('seq', 'head')), may hold values from -0.1875 to 0.1875
Outputs:
- latent_out: bfloat16 [4, 1024, 1024], P('head', 'seq')
Inputs may be any that keep to these rules, and one draw needn't show every extreme that they name: Latent i of row b stands at context position offsets[b] + i.
All inputs are finite; a program needn't handle non-finite values.
Results may differ from a plain program's by a relative error of at most 0.013.
Values may be sent and summed in bfloat16 or wider, within the bound.
No kernel may reach another device: no remote copies, remote signals or barrier semaphores. Data moves between devices by JAX's collectives and lax.ppermute only.
A program may use at most 128 MiB of HBM per device.

v0:
```python
import jax
import jax.numpy as jnp
from jax import lax
from jax.sharding import PartitionSpec as P

H = 16
EPSILON = 1e-06
NEGATIVE = -1e30


def rms_norm(value_matrix, gain):
    value_matrix = value_matrix.astype(jnp.float32)
    scale = lax.rsqrt(jnp.mean(value_matrix * value_matrix, axis=-1, keepdims=True) + EPSILON)
    return (value_matrix * scale * gain).astype(jnp.bfloat16)


def project(left, weight):
    return jnp.einsum("...k,kn->...n", left, weight, preferred_element_type=jnp.float32)


def block_scores(query_row_block, key_rows, query_pos, key_base, start, key_span, scale):
    key_tile = lax.dynamic_slice_in_dim(key_rows, start, key_span, 0)
    score_matrix = (
        jnp.einsum("oqi,cqi->qoc", query_row_block, key_tile, preferred_element_type=jnp.float32)
        * scale
    )
    key_pos = key_base + start + jnp.arange(key_span, dtype=jnp.int32)
    valid = key_pos[None, None, :] <= query_pos[None, :, None]
    return (jnp.where(valid, score_matrix, NEGATIVE), valid)


def causal_top(query_row_block, key_rows, query_pos, key_base, key_span, scale):

    def advance(index, best):
        start = index * key_span

        def compute(kept):
            score_matrix, valid = block_scores(
                query_row_block, key_rows, query_pos, key_base, start, key_span, scale
            )
            return jnp.maximum(kept, jnp.max(score_matrix, axis=2))

        result = compute(best)
        return result

    initial = jnp.full((query_row_block.shape[1], query_row_block.shape[0]), NEGATIVE, jnp.float32)
    return lax.fori_loop(0, key_rows.shape[0] // key_span, advance, initial)


def causal_sums(
    query_row_block, key_rows, value_rows, row_top, query_pos, key_base, key_span, scale
):

    def advance(index, carry):
        start = index * key_span

        def compute(kept):
            numerator_sum, denom = kept
            score_matrix, valid = block_scores(
                query_row_block, key_rows, query_pos, key_base, start, key_span, scale
            )
            probability_rows = jnp.where(
                valid, jnp.exp(score_matrix - row_top[:, :, None]), 0.0
            ).astype(jnp.bfloat16)
            value_tile = lax.dynamic_slice_in_dim(value_rows, start, key_span, 0)
            numerator_sum = numerator_sum + jnp.einsum(
                "ycv,vys->cys", probability_rows, value_tile, preferred_element_type=jnp.float32
            )
            denom = denom + jnp.transpose(jnp.sum(probability_rows.astype(jnp.float32), axis=2))
            return (numerator_sum, denom)

        result = compute(carry)
        return result

    count, heads, head_width = query_row_block.shape
    initial = (
        jnp.zeros((count, heads, head_width), jnp.float32),
        jnp.zeros((count, heads), jnp.float32),
    )
    return lax.fori_loop(0, key_rows.shape[0] // key_span, advance, initial)


def latent_attention(piece):
    count = piece.shape[1]
    head_width = piece.shape[-1]
    query_matrix = piece[:, :, 0]
    key_matrix = piece[:, :, 1]
    value_matrix = piece[:, :, 2]
    score_matrix = jnp.einsum(
        "bmhd,bkhd->bhmk", query_matrix, key_matrix, preferred_element_type=jnp.float32
    ) * head_width ** (-0.5)
    positions = jnp.arange(count, dtype=jnp.int32)
    valid = positions[None, :] <= positions[:, None]
    score_matrix = jnp.where(valid, score_matrix, NEGATIVE)
    row_top = jnp.max(score_matrix, axis=3, keepdims=True)
    probability_rows = jnp.where(valid, jnp.exp(score_matrix - row_top), 0.0).astype(jnp.bfloat16)
    denom = jnp.sum(probability_rows.astype(jnp.float32), axis=3)
    numerator_sum = jnp.einsum(
        "bhmk,bkhd->bmhd", probability_rows, value_matrix, preferred_element_type=jnp.float32
    )
    return (numerator_sum / jnp.transpose(denom, (0, 2, 1))[:, :, :, None]).astype(jnp.bfloat16)


def per_device(
    context,
    latents,
    offsets,
    query_gain,
    key_gain,
    layer_gain,
    cross_query,
    cross_key,
    cross_value,
    cross_out,
    layer_qkv,
    layer_out,
):
    batch, ctx_len, width = context.shape
    latent_count = latents.shape[1]
    heads = H
    head_width = width // heads
    groups = lax.axis_size("seq")
    local_rows = latent_count // groups
    group_heads = heads // groups
    seq_index = lax.axis_index("seq")
    scale = head_width ** (-0.5)
    gathered = (
        lax.all_gather(cross_query, ("seq", "head"), axis=0, tiled=True),
        lax.all_gather(cross_key, ("seq", "head"), axis=0, tiled=True),
        lax.all_gather(cross_value, ("seq", "head"), axis=0, tiled=True),
        lax.all_gather(cross_out, ("seq", "head"), axis=0, tiled=True),
        lax.all_gather(layer_qkv, ("seq", "head"), axis=1, tiled=True),
        lax.all_gather(layer_out, ("seq", "head"), axis=1, tiled=True),
    )
    normed_latents = rms_norm(latents, query_gain)
    query_matrix = project(normed_latents, gathered[0])
    query_matrix = query_matrix.astype(jnp.bfloat16)
    normed_context = rms_norm(context, key_gain)
    key_matrix = project(normed_context, gathered[1])
    value_matrix = project(normed_context, gathered[2])
    key_matrix = key_matrix.astype(jnp.bfloat16).reshape(batch, ctx_len, heads, head_width)
    value_matrix = value_matrix.astype(jnp.bfloat16).reshape(batch, ctx_len, heads, head_width)
    query_head_rows = query_matrix.reshape(batch, latent_count, heads, head_width)
    query_pos = offsets[:, None] + jnp.arange(latent_count, dtype=jnp.int32)[None, :]
    key_groups, value_groups = (
        lax.all_to_all(key_matrix, "seq", split_axis=2, concat_axis=1, tiled=True),
        lax.all_to_all(value_matrix, "seq", split_axis=2, concat_axis=1, tiled=True),
    )
    query_groups = lax.dynamic_slice_in_dim(
        query_head_rows, seq_index * group_heads, group_heads, 2
    )
    total_len = key_groups.shape[1]
    key_span = max(min(total_len, 512), total_len // 16)
    row_top = causal_top(query_groups[0], key_groups[0], query_pos[0], 0, key_span, scale)
    numerator_sum, denom = causal_sums(
        query_groups[0], key_groups[0], value_groups[0], row_top, query_pos[0], 0, key_span, scale
    )
    results = [(numerator_sum / denom[:, :, None]).astype(jnp.bfloat16)]
    attended = lax.all_to_all(
        jnp.stack(results), "seq", split_axis=1, concat_axis=2, tiled=True
    ).reshape(batch, local_rows, width)
    latents_own = lax.dynamic_slice_in_dim(latents, seq_index * local_rows, local_rows, 1)
    update = project(attended, gathered[3])
    hidden = (latents_own.astype(jnp.float32) + update).astype(jnp.bfloat16)
    for layer in range(layer_qkv.shape[0]):
        normed = rms_norm(hidden, layer_gain[layer])
        qkv = project(normed, gathered[4][layer])
        grouped = qkv.astype(jnp.bfloat16).reshape(batch, local_rows, 3, heads, head_width)
        mixed = latent_attention(
            lax.all_to_all(grouped, "seq", split_axis=3, concat_axis=1, tiled=True)
        )
        merged = lax.all_to_all(mixed, "seq", split_axis=1, concat_axis=2, tiled=True).reshape(
            batch, local_rows, width
        )
        update = project(merged, gathered[5][layer])
        hidden = (hidden.astype(jnp.float32) + update).astype(jnp.bfloat16)
    return hidden


def solution(mesh):
    return jax.shard_map(
        per_device,
        mesh=mesh,
        in_specs=(
            P("head", "seq", None),
            P("head", None, None),
            P("head"),
            P(),
            P(),
            P(),
            P(("seq", "head"), None),
            P(("seq", "head"), None),
            P(("seq", "head"), None),
            P(("seq", "head"), None),
            P(None, ("seq", "head"), None),
            P(None, ("seq", "head"), None),
        ),
        out_specs=P("head", "seq", None),
        check_vma=False,
    )
```

profile of v0, /device:TPU:0, one launch (start us, length us, event | category | flops | bytes accessed | tf_op | source)
XLA Modules:
  0.0 485.0 jit_solution(4928080488201104973)
XLA Ops:
  9.9 1.5 fusion.33
  11.4 57.8 %all-gather.9.cloned.1.call-done = bf16[1024,1024]{1,0:T(8,128)(2,1)} async-done(((bf16[32,1024]{1,0:T(8,128)(2,1)}), bf16[1024,1024]{1,0:T(8,128)(2,1)}) %all-gather.9.cloned.1.call-update) | async-done | bytes 2097168 | tf_op jit(solution)/shard_map/all_gather | solution.py:129
  69.2 3.2 convolution_convert_fusion
  73.8 4.3 all-to-all-start.1
  78.7 2.1 fusion.22
  80.8 51.9 %all-gather.7.cloned.1.call-done = bf16[1024,1024]{1,0:T(8,128)(2,1)} async-done(((bf16[32,1024]{1,0:T(8,128)(2,1)}), bf16[1024,1024]{1,0:T(8,128)(2,1)}) %all-gather.7.cloned.1.call-update) | async-done | bytes 2097168 | tf_op jit(solution)/shard_map/all_gather | solution.py:130
  132.7 3.9 convolution_convert_fusion.1
  136.6 2.3 copy.70
  138.9 51.8 %all-gather.11.cloned.1.call-done = bf16[1024,1024]{1,0:T(8,128)(2,1)} async-done(((bf16[32,1024]{1,0:T(8,128)(2,1)}), bf16[1024,1024]{1,0:T(8,128)(2,1)}) %all-gather.11.cloned.1.call-update) | async-done | bytes 2097168 | tf_op jit(solution)/shard_map/all_gather | solution.py:128
  190.7 4.8 fusion.43
  195.5 4.3 all-to-all-start
  199.9 1.6 copy.75
  201.4 1.6 squeeze.30
  203.0 16.9 %while.30 = (s32[]{:T(128)}, f32[2,1024]{1,0:T(2,128)S(1)}, bf16[4096,2,64]{0,2,1:T(8,128)(2,1)S(1)}, bf16[1024,2,64]{0,2,1:T(8,128)(2,1)S(1)}, s32[]{:T(128)}, ...) while((s32[]{:T(128)}, f32[2,1024]{1,0:T(2,128)S(1)}, bf16[4096,2,64]{0,2,1:T(8,128)(2,1)S(1)}, ...), condition=%wide.region_4.5_spmd.clone, body=%wide.region_2.4_spmd.clone.sunk | while | flops 137891328 | bytes 1487009 | solution.py:47
  219.9 8.5 %all-to-all-done = bf16[1,512,16,64]{1,3,0,2:T(8,128)(2,1)S(1)} async-done(((bf16[1,512,16,64]{1,3,0,2:T(8,128)(2,1)}), bf16[1,512,16,64]{1,3,0,2:T(8,128)(2,1)S(1)}, u32[]{:S(2)}, u32[]{:S(2)}) %all-to-all-start) | async-done | bytes 1048608 | tf_op jit(solution)/shard_map/all_to_all | solution.py:147
  230.2 40.6 %while.31 = (s32[]{:T(128)}, f32[1024,2,64]{0,2,1:T(8,128)S(1)}, f32[1024,2]{0,1:T(2,128)S(1)}, bf16[4096,2,64]{0,2,1:T(8,128)(2,1)}, bf16[4096,2,64]{0,2,1:T(8,...) while((s32[]{:T(128)}, f32[1024,2,64]{0,2,1:T(8,128)S(1)}, ...), condition=%wide.region_7.8_spmd.clone, body=%wide.region_5.7_spmd.clone.sunk | while | flops 276565504 | bytes 6869182 | solution.py:80
  231.3 2.5 convert_reduce_fusion.4
  236.3 2.5 convert_reduce_fusion.4
  238.9 1.5 fusion.107
  241.5 2.5 convert_reduce_fusion.4
  244.0 1.4 fusion.107
  246.5 2.5 convert_reduce_fusion.4
  249.1 1.4 fusion.107
  251.6 2.5 convert_reduce_fusion.4
  254.1 1.4 fusion.107
  256.7 2.5 convert_reduce_fusion.4
  259.2 1.4 fusion.107
  261.7 2.5 convert_reduce_fusion.4
  264.3 1.5 fusion.107
  266.8 2.5 convert_reduce_fusion.4
  272.7 3.5 all-to-all-start.2
  276.3 9.1 %all-to-all-done.2 = bf16[8,2,8192]{2,1,0:T(2,128)(2,1)S(1)} async-done(((bf16[8,2,8192]{2,1,0:T(2,128)(2,1)}), bf16[8,2,8192]{2,1,0:T(2,128)(2,1)S(1)}, u32[]{:S(2)}, u32[]{:S(2)}) %all-to-all-start.2) | async-done | bytes 262176 | tf_op jit(solution)/shard_map/all_to_all | solution.py:159
  286.1 2.1 multiply_reduce_fusion.1
  288.3 64.0 %all-gather.15.cloned.1.call-done = bf16[2,1024,3072]{2,1,0:T(8,128)(2,1)} async-done(((bf16[2,32,3072]{2,1,0:T(8,128)(2,1)}), bf16[2,1024,3072]{2,1,0:T(8,128)(2,1)}) %all-gather.15.cloned.1.call-update) | async-done | bytes 12582928 | tf_op jit(solution)/shard_map/all_gather | solution.py:132
  352.3 3.8 fusion.31
  357.4 4.0 all-to-all-start.3
  361.8 23.0 %all-to-all-done.3 = bf16[1,128,3,16,64]{1,4,2,0,3:T(8,128)(2,1)S(1)} async-done(((bf16[1,128,3,16,64]{1,4,2,0,3:T(8,128)(2,1)}), bf16[1,128,3,16,64]{1,4,2,0,3:T(8,128)(2,1)S(1)}, u32[]{:S(2)}, u32[]{:S(2)}) %all-to-all-start.3) | async-done | bytes 786464 | tf_op jit(solution)/shard_map/all_to_all | solution.py:170
  385.6 6.0 %convert_reduce_fusion.2 = (f32[2,1024]{1,0:T(2,128)S(1)}, bf16[2,1024,1024]{1,2,0:T(8,128)(2,1)}) fusion(pred[1024,1024]{0,1:T(8,128)(4,1)S(1)} %iota_compare_fusion, bf16[1,1024,3,2,64]{1,4,3,2,0:T(8,128)(2,1)S(1)} %all_to_all.93), kind=kOutput, calls=%fused_computation.31 | convolution fusion | flops 283116544 | bytes 6823936 | tf_op jit(solution)/shard_map/sub | solution.py:96
  391.6 3.0 fusion.57
  395.5 18.1 %all_to_all.111 = bf16[8,2,8192]{2,1,0:T(2,128)(2,1)S(1)} all-to-all(bf16[8,2,8192]{2,1,0:T(2,128)(2,1)S(1)} %reshape.309), channel_id=1, replica_groups=mesh['seq'=8,'head'=4] {'seq'}, dimensions={0} | all-to-all | bytes 524288 | tf_op jit(solution)/shard_map/all_to_all | solution.py:172
  414.2 6.9 %all-gather.17.cloned.1.call-done = bf16[2,1024,1024]{2,1,0:T(8,128)(2,1)} async-done(((bf16[2,32,1024]{2,1,0:T(8,128)(2,1)}), bf16[2,1024,1024]{2,1,0:T(8,128)(2,1)}) %all-gather.17.cloned.1.call-update) | async-done | bytes 4194320 | tf_op jit(solution)/shard_map/all_gather | solution.py:133
  421.1 2.1 multiply_reduce_fusion
  423.3 3.8 fusion.32
  427.6 24.1 %all_to_all.112 = bf16[1,128,3,16,64]{1,4,2,0,3:T(8,128)(2,1)S(1)} all-to-all(bf16[1,128,3,16,64]{1,4,2,0,3:T(8,128)(2,1)S(1)} %copy.89), channel_id=1, replica_groups=mesh['seq'=8,'head'=4] {'seq'}, dimensions={3} | all-to-all | bytes 1572864 | tf_op jit(solution)/shard_map/all_to_all | solution.py:170
  452.5 6.0 %convert_reduce_fusion.1 = (f32[2,1024]{1,0:T(2,128)S(1)}, bf16[2,1024,1024]{1,2,0:T(8,128)(2,1)}) fusion(pred[1024,1024]{0,1:T(8,128)(4,1)S(1)} %iota_compare_fusion, bf16[1,1024,3,2,64]{1,4,3,2,0:T(8,128)(2,1)S(1)} %all_to_all.100), kind=kOutput, calls=%fused_computation.28 | convolution fusion | flops 283116544 | bytes 6823936 | tf_op jit(solution)/shard_map/sub | solution.py:96
  458.5 3.0 fusion.59
  462.4 12.3 %all_to_all.113 = bf16[8,2,8192]{2,1,0:T(2,128)(2,1)S(1)} all-to-all(bf16[8,2,8192]{2,1,0:T(2,128)(2,1)S(1)} %reshape.311), channel_id=1, replica_groups=mesh['seq'=8,'head'=4] {'seq'}, dimensions={0} | all-to-all | bytes 524288 | tf_op jit(solution)/shard_map/all_to_all | solution.py:172
  475.4 2.8 fusion.55
  (136 shorter events, 44.0 us)
Async XLA Ops:
  6.5 62.7 %all-gather.9.cloned.1.call-start = ((), (), s32[]{:S(2)}) async-start(), calls=%async_computation.8 | async-start | bytes 2162688 | tf_op jit(solution)/shard_map/all_gather | solution.py:129
  7.3 125.4 %all-gather.7.cloned.1.call-start = ((), (), s32[]{:S(2)}) async-start(), calls=%async_computation.7 | async-start | bytes 2162688 | tf_op jit(solution)/shard_map/all_gather | solution.py:130
  8.0 182.7 %all-gather.11.cloned.1.call-start = ((), (), s32[]{:S(2)}) async-start(), calls=%async_computation.9 | async-start | bytes 2162688 | tf_op jit(solution)/shard_map/all_gather | solution.py:128
  8.7 277.4 %all-gather.13.cloned.1.call-start = ((), (), s32[]{:S(2)}) async-start(), calls=%async_computation.10 | async-start | bytes 2162688 | tf_op jit(solution)/shard_map/all_gather | solution.py:131
  9.3 343.0 %all-gather.15.cloned.1.call-start = ((), (), s32[]{:S(2)}) async-start(), calls=%async_computation.11 | async-start | bytes 12976128 | tf_op jit(solution)/shard_map/all_gather | solution.py:132
  72.4 60.3 %copy-start = (bf16[1,512,1024]{2,1,0:T(8,128)(2,1)S(1)}, bf16[1,512,1024]{2,1,0:T(8,128)(2,1)}, u32[]{:S(2)}) copy-start(bf16[1,512,1024]{2,1,0:T(8,128)(2,1)} %param.16) | copy-start | bytes 3145732
  72.4 60.2 %copy-start.3 = (f32[1024]{0:T(1024)S(1)}, f32[1024]{0:T(1024)}, u32[]{:S(2)}) copy-start(f32[1024]{0:T(1024)} %param.20) | copy-start | bytes 12292
  73.8 121.7 %all-to-all-start.1 = ((bf16[1,512,16,64]{1,3,0,2:T(8,128)(2,1)}), bf16[1,512,16,64]{1,3,0,2:T(8,128)(2,1)S(1)}, u32[]{:S(2)}, u32[]{:S(2)}) async-start(bf16[1,512,16,64]{1,3,0,2:T(8,128)(2,1)} %bitcast.6), calls=%async_computation.1 | async-start | bytes 2097152 | tf_op jit(solution)/shard_map/all_to_all | solution.py:146
  78.1 343.1 %all-gather.17.cloned.1.call-start = ((), (), s32[]{:S(2)}) async-start(), calls=%async_computation.12 | async-start | bytes 4325376 | tf_op jit(solution)/shard_map/all_gather | solution.py:133
  80.8 109.9 %copy-start.4 = (f32[1024]{0:T(1024)S(1)}, f32[1024]{0:T(1024)}, u32[]{:S(2)}) copy-start(f32[1024]{0:T(1024)} %param.19) | copy-start | bytes 12292
  195.5 32.8 %all-to-all-start = ((bf16[1,512,16,64]{1,3,0,2:T(8,128)(2,1)}), bf16[1,512,16,64]{1,3,0,2:T(8,128)(2,1)S(1)}, u32[]{:S(2)}, u32[]{:S(2)}) async-start(bf16[1,512,16,64]{1,3,0,2:T(8,128)(2,1)} %bitcast.2), calls=%async_computation | async-start | bytes 2097152 | tf_op jit(solution)/shard_map/all_to_all | solution.py:147
  219.8 8.5 %copy-start.1 = (bf16[4096,2,64]{0,2,1:T(8,128)(2,1)}, bf16[4096,2,64]{0,2,1:T(8,128)(2,1)S(1)}, u32[]{:S(2)}) copy-start(bf16[4096,2,64]{0,2,1:T(8,128)(2,1)S(1)} %get-tuple-element.490) | copy-start | bytes 3145732
  230.2 46.0 %copy-start.2 = (f32[2,1024]{1,0:T(2,128)S(1)}, f32[2,1024]{1,0:T(2,128)}, u32[]{:S(2)}) copy-start(f32[2,1024]{1,0:T(2,128)} %param.21) | copy-start | bytes 24580
  272.7 12.7 %all-to-all-start.2 = ((bf16[8,2,8192]{2,1,0:T(2,128)(2,1)}), bf16[8,2,8192]{2,1,0:T(2,128)(2,1)S(1)}, u32[]{:S(2)}, u32[]{:S(2)}) async-start(bf16[8,2,8192]{2,1,0:T(2,128)(2,1)} %reshape.307), calls=%async_computation.2 | async-start | bytes 524288 | tf_op jit(solution)/shard_map/all_to_all | solution.py:159
  357.4 27.3 %all-to-all-start.3 = ((bf16[1,128,3,16,64]{1,4,2,0,3:T(8,128)(2,1)}), bf16[1,128,3,16,64]{1,4,2,0,3:T(8,128)(2,1)S(1)}, u32[]{:S(2)}, u32[]{:S(2)}) async-start(bf16[1,128,3,16,64]{1,4,2,0,3:T(8,128)(2,1)} %copy.82), calls=%async_computation.3 | async-start | bytes 1572864 | tf_op jit(solution)/shard_map/all_to_all | solution.py:170
Sparse Core Ops, SparseCore 0:
  10.2 58.9 all-gather.8
  72.0 60.5 all-gather.6
  135.5 55.0 all-gather.10
  193.4 61.0 all-gather.12
  257.3 94.9 all-gather.14
  355.1 66.0 all-gather.16
where the time goes:
time: 486 us; the launch traced here: 485 us
  waiting for transfers between devices  277 us (57%)
  matrix products  84.7 us (17%)
  blocking collectives  54.5 us (11%)
  other arithmetic  20.5 us (4%)
  local copies, waits for them, and re-layouts  17.5 us (4%)
  starting transfers between devices  16.4 us (3%)
  between operations  13.8 us (3%)
    all_gather x1, waiting for transfers between devices, per_device(): lax.all_gather(layer_qkv, ('seq', 'head'), axis=1, tiled=True)  64 us
    all_gather x1, waiting for transfers between devices, per_device(): lax.all_gather(cross_key, ('seq', 'head'), axis=0, tiled=True)  57.8 us
    all_gather x1, waiting for transfers between devices, per_device(): lax.all_gather(cross_value, ('seq', 'head'), axis=0, tiled=True)  51.9 us
    all_gather x1, waiting for transfers between devices, per_device(): lax.all_gather(cross_query, ('seq', 'head'), axis=0, tiled=True)  51.8 us
    all_to_all x2, blocking collectives, per_device(): lax.all_to_all(mixed, 'seq', split_axis=1, concat_axis=2, tiled=True)  30.4 us
    dot_general x16, matrix products, block_scores(): jnp.einsum('oqi,cqi->qoc', query_row_block, key_tile, preferred_element_t...  28.3 us
    dot_general x8, matrix products, project(): jnp.einsum('...k,kn->...n', left, weight, preferred_element_type=jnp.floa...  26.6 us
    all_to_all x1, blocking collectives, per_device(): lax.all_to_all(grouped, 'seq', split_axis=3, concat_axis=1, tiled=True)  24.1 us
  transfers between devices with their start and end apart: 10, of which 8 were waited for; matrix products, arithmetic and copies ran while one was open for 21% of the time, Pallas kernels for 0%

commit v1 on v0

--- a/solution.py
+++ b/solution.py
@@ -6,6 +6,13 @@
 H = 16
 EPSILON = 1e-06
 NEGATIVE = -1e30
+
+
+def stacked_exchange(array, axis, split, join):
+    peers = lax.axis_size(axis)
+    blocks = jnp.stack(jnp.split(array, peers, axis=split), axis=0)
+    blocks = lax.all_to_all(blocks, axis, split_axis=0, concat_axis=0)
+    return jnp.concatenate(blocks, axis=join)
 
 
 def rms_norm(value_matrix, gain):
@@ -169,9 +176,7 @@
         mixed = latent_attention(
             lax.all_to_all(grouped, "seq", split_axis=3, concat_axis=1, tiled=True)
         )
-        merged = lax.all_to_all(mixed, "seq", split_axis=1, concat_axis=2, tiled=True).reshape(
-            batch, local_rows, width
-        )
+        merged = stacked_exchange(mixed, "seq", 1, 2).reshape(batch, local_rows, width)
         update = project(merged, gathered[5][layer])
         hidden = (hidden.astype(jnp.float32) + update).astype(jnp.bfloat16)
     return hidden

time: 486 us -> 486 us (level)
  blocking collectives: 54.5 us -> 36.4 us
  waiting for transfers between devices: 277 us -> 290 us
    all_to_all x2 -> x1, blocking collectives: 30.4 us -> 12.3 us  [stacked_exchange(): blocks = lax.all_to_all(blocks, axis, split_axis=0, concat_axis=0)]
    all_gather x1, waiting for transfers between devices: 6.91 us -> 19.9 us  [per_device(): lax.all_gather(layer_out, ('seq', 'head'), axis=1, tiled=True)]
  transfers between devices with their start and end apart: 10 -> 11, of which waited for: 8 -> 8; matrix products, arithmetic and copies ran while one was open for 21% -> 22% of each run, Pallas kernels for 0% -> 0%
where the time goes in v1:
time: 486 us; the launch traced here: 484 us
  waiting for transfers between devices  290 us (60%)
  matrix products  83.2 us (17%)
  blocking collectives  36.4 us (7%)
  other arithmetic  20.5 us (4%)
  starting transfers between devices  20 us (4%)
  local copies, waits for them, and re-layouts  19.8 us (4%)
  between operations  13.8 us (3%)
    all_gather x1, waiting for transfers between devices, per_device(): lax.all_gather(layer_qkv, ('seq', 'head'), axis=1, tiled=True)  64.2 us
    all_gather x1, waiting for transfers between devices, per_device(): lax.all_gather(cross_key, ('seq', 'head'), axis=0, tiled=True)  57.8 us
    all_gather x1, waiting for transfers between devices, per_device(): lax.all_gather(cross_value, ('seq', 'head'), axis=0, tiled=True)  51.9 us
    all_gather x1, waiting for transfers between devices, per_device(): lax.all_gather(cross_query, ('seq', 'head'), axis=0, tiled=True)  51.8 us
    dot_general x16, matrix products, block_scores(): jnp.einsum('oqi,cqi->qoc', query_row_block, key_tile, preferred_element_t...  28.4 us
    dot_general x8, matrix products, project(): jnp.einsum('...k,kn->...n', left, weight, preferred_element_type=jnp.floa...  25 us
    all_to_all x1, blocking collectives, per_device(): lax.all_to_all(grouped, 'seq', split_axis=3, concat_axis=1, tiled=True)  24.1 us
    all_to_all x1, waiting for transfers between devices, per_device(): lax.all_to_all(grouped, 'seq', split_axis=3, concat_axis=1, tiled=True)  23 us
  transfers between devices with their start and end apart: 11, of which 8 were waited for; matrix products, arithmetic and copies ran while one was open for 22% of the time, Pallas kernels for 0%

profile of v1, /device:TPU:0, one launch (start us, length us, event | category | flops | bytes accessed | tf_op | source)
XLA Modules:
  0.0 484.5 jit_solution(5945957646295921035)
XLA Ops:
  9.9 1.5 fusion.33
  11.4 57.8 %all-gather.9.cloned.1.call-done = bf16[1024,1024]{1,0:T(8,128)(2,1)} async-done(((bf16[32,1024]{1,0:T(8,128)(2,1)}), bf16[1024,1024]{1,0:T(8,128)(2,1)}) %all-gather.9.cloned.1.call-update) | async-done | bytes 2097168 | tf_op jit(solution)/shard_map/all_gather | solution.py:136
  69.2 3.2 convolution_convert_fusion
  73.8 4.3 all-to-all-start.1
  78.7 2.1 fusion.22
  80.8 51.9 %all-gather.7.cloned.1.call-done = bf16[1024,1024]{1,0:T(8,128)(2,1)} async-done(((bf16[32,1024]{1,0:T(8,128)(2,1)}), bf16[1024,1024]{1,0:T(8,128)(2,1)}) %all-gather.7.cloned.1.call-update) | async-done | bytes 2097168 | tf_op jit(solution)/shard_map/all_gather | solution.py:137
  132.7 3.9 convolution_convert_fusion.1
  136.6 2.3 copy.44
  138.8 51.8 %all-gather.11.cloned.1.call-done = bf16[1024,1024]{1,0:T(8,128)(2,1)} async-done(((bf16[32,1024]{1,0:T(8,128)(2,1)}), bf16[1024,1024]{1,0:T(8,128)(2,1)}) %all-gather.11.cloned.1.call-update) | async-done | bytes 2097168 | tf_op jit(solution)/shard_map/all_gather | solution.py:135
  190.7 4.8 fusion.43
  195.5 4.3 all-to-all-start
  199.8 1.6 copy.49
  201.4 1.6 squeeze.30
  203.0 16.9 %while.30 = (s32[]{:T(128)}, f32[2,1024]{1,0:T(2,128)S(1)}, bf16[4096,2,64]{0,2,1:T(8,128)(2,1)S(1)}, bf16[1024,2,64]{0,2,1:T(8,128)(2,1)S(1)}, s32[]{:T(128)}, ...) while((s32[]{:T(128)}, f32[2,1024]{1,0:T(2,128)S(1)}, bf16[4096,2,64]{0,2,1:T(8,128)(2,1)S(1)}, ...), condition=%wide.region_4.5_spmd.clone, body=%wide.region_2.4_spmd.clone.sunk | while | flops 137891328 | bytes 1487009 | solution.py:54
  219.8 8.5 %all-to-all-done = bf16[1,512,16,64]{1,3,0,2:T(8,128)(2,1)S(1)} async-done(((bf16[1,512,16,64]{1,3,0,2:T(8,128)(2,1)}), bf16[1,512,16,64]{1,3,0,2:T(8,128)(2,1)S(1)}, u32[]{:S(2)}, u32[]{:S(2)}) %all-to-all-start) | async-done | bytes 1048608 | tf_op jit(solution)/shard_map/all_to_all | solution.py:154
  230.2 40.6 %while.31 = (s32[]{:T(128)}, f32[1024,2,64]{0,2,1:T(8,128)S(1)}, f32[1024,2]{0,1:T(2,128)S(1)}, bf16[4096,2,64]{0,2,1:T(8,128)(2,1)}, bf16[4096,2,64]{0,2,1:T(8,...) while((s32[]{:T(128)}, f32[1024,2,64]{0,2,1:T(8,128)S(1)}, ...), condition=%wide.region_7.8_spmd.clone, body=%wide.region_5.7_spmd.clone.sunk | while | flops 276565504 | bytes 6869182 | solution.py:87
  231.3 2.5 convert_reduce_fusion.4
  233.8 1.4 fusion.107
  236.3 2.5 convert_reduce_fusion.4
  238.9 1.5 fusion.107
  241.5 2.5 convert_reduce_fusion.4
  244.0 1.4 fusion.107
  246.5 2.5 convert_reduce_fusion.4
  249.1 1.4 fusion.107
  251.6 2.5 convert_reduce_fusion.4
  254.1 1.4 fusion.107
  256.7 2.5 convert_reduce_fusion.4
  259.2 1.4 fusion.107
  261.7 2.5 convert_reduce_fusion.4
  264.3 1.5 fusion.107
  266.8 2.5 convert_reduce_fusion.4
  272.7 3.5 all-to-all-start.2
  276.3 9.1 %all-to-all-done.2 = bf16[8,2,8192]{2,1,0:T(2,128)(2,1)S(1)} async-done(((bf16[8,2,8192]{2,1,0:T(2,128)(2,1)}), bf16[8,2,8192]{2,1,0:T(2,128)(2,1)S(1)}, u32[]{:S(2)}, u32[]{:S(2)}) %all-to-all-start.2) | async-done | bytes 262176 | tf_op jit(solution)/shard_map/all_to_all | solution.py:166
  286.1 2.1 multiply_reduce_fusion.1
  288.3 64.2 %all-gather.15.cloned.1.call-done = bf16[2,1024,3072]{2,1,0:T(8,128)(2,1)} async-done(((bf16[2,32,3072]{2,1,0:T(8,128)(2,1)}), bf16[2,1024,3072]{2,1,0:T(8,128)(2,1)}) %all-gather.15.cloned.1.call-update) | async-done | bytes 12582928 | tf_op jit(solution)/shard_map/all_gather | solution.py:139
  352.5 3.8 fusion.31
  357.6 4.0 all-to-all-start.3
  362.0 23.0 %all-to-all-done.3 = bf16[1,128,3,16,64]{1,4,2,0,3:T(8,128)(2,1)S(1)} async-done(((bf16[1,128,3,16,64]{1,4,2,0,3:T(8,128)(2,1)}), bf16[1,128,3,16,64]{1,4,2,0,3:T(8,128)(2,1)S(1)}, u32[]{:S(2)}, u32[]{:S(2)}) %all-to-all-start.3) | async-done | bytes 786464 | tf_op jit(solution)/shard_map/all_to_all | solution.py:177
  385.8 6.0 %convert_reduce_fusion.2 = (f32[2,1024]{1,0:T(2,128)S(1)}, bf16[2,1024,1024]{1,2,0:T(8,128)(2,1)}) fusion(pred[1024,1024]{0,1:T(8,128)(4,1)S(1)} %iota_compare_fusion, bf16[1,1024,3,2,64]{1,4,3,2,0:T(8,128)(2,1)S(1)} %all_to_all.77), kind=kOutput, calls=%fused_computation.31 | convolution fusion | flops 283116544 | bytes 6823936 | tf_op jit(solution)/shard_map/sub | solution.py:103
  391.8 3.0 fusion.57
  399.9 3.6 all-to-all-start.4
  403.5 19.9 %all-gather.17.cloned.1.call-done = bf16[2,1024,1024]{2,1,0:T(8,128)(2,1)} async-done(((bf16[2,32,1024]{2,1,0:T(8,128)(2,1)}), bf16[2,1024,1024]{2,1,0:T(8,128)(2,1)}) %all-gather.17.cloned.1.call-update) | async-done | bytes 4194320 | tf_op jit(solution)/shard_map/all_gather | solution.py:140
  423.4 2.1 multiply_reduce_fusion
  425.5 3.8 fusion.32
  429.8 24.1 %all_to_all.91 = bf16[1,128,3,16,64]{1,4,2,0,3:T(8,128)(2,1)S(1)} all-to-all(bf16[1,128,3,16,64]{1,4,2,0,3:T(8,128)(2,1)S(1)} %copy.60), channel_id=1, replica_groups=mesh['seq'=8,'head'=4] {'seq'}, dimensions={3} | all-to-all | bytes 1572864 | tf_op jit(solution)/shard_map/all_to_all | solution.py:177
  454.8 6.0 %convert_reduce_fusion.1 = (f32[2,1024]{1,0:T(2,128)S(1)}, bf16[2,1024,1024]{1,2,0:T(8,128)(2,1)}) fusion(pred[1024,1024]{0,1:T(8,128)(4,1)S(1)} %iota_compare_fusion, bf16[1,1024,3,2,64]{1,4,3,2,0:T(8,128)(2,1)S(1)} %all_to_all.82), kind=kOutput, calls=%fused_computation.28 | convolution fusion | flops 283116544 | bytes 6823936 | tf_op jit(solution)/shard_map/sub | solution.py:103
  460.7 3.2 fusion.59
  464.1 12.3 %all_to_all.92 = bf16[8,1,128,2,64]{2,4,3,1,0:T(8,128)(2,1)S(1)} all-to-all(bf16[8,1,128,2,64]{2,4,3,1,0:T(8,128)(2,1)S(1)} %constant_dynamic-update-slice_fusion.8), channel_id=1, replica_groups=mesh['seq'=8,'head'=4] {'seq'}, dimensions={0} | all-to-all | bytes 524288 | tf_op jit(solution)/shard_map/all_to_all | solution.py:14
  (145 shorter events, 46.0 us)
Async XLA Ops:
  6.5 62.7 %all-gather.9.cloned.1.call-start = ((), (), s32[]{:S(2)}) async-start(), calls=%async_computation.8 | async-start | bytes 2162688 | tf_op jit(solution)/shard_map/all_gather | solution.py:136
  7.3 125.4 %all-gather.7.cloned.1.call-start = ((), (), s32[]{:S(2)}) async-start(), calls=%async_computation.7 | async-start | bytes 2162688 | tf_op jit(solution)/shard_map/all_gather | solution.py:137
  8.0 182.6 %all-gather.11.cloned.1.call-start = ((), (), s32[]{:S(2)}) async-start(), calls=%async_computation.9 | async-start | bytes 2162688 | tf_op jit(solution)/shard_map/all_gather | solution.py:135
  8.7 277.3 %all-gather.13.cloned.1.call-start = ((), (), s32[]{:S(2)}) async-start(), calls=%async_computation.10 | async-start | bytes 2162688 | tf_op jit(solution)/shard_map/all_gather | solution.py:138
  9.3 343.2 %all-gather.15.cloned.1.call-start = ((), (), s32[]{:S(2)}) async-start(), calls=%async_computation.11 | async-start | bytes 12976128 | tf_op jit(solution)/shard_map/all_gather | solution.py:139
  72.4 60.2 %copy-start.1 = (bf16[1,512,1024]{2,1,0:T(8,128)(2,1)S(1)}, bf16[1,512,1024]{2,1,0:T(8,128)(2,1)}, u32[]{:S(2)}) copy-start(bf16[1,512,1024]{2,1,0:T(8,128)(2,1)} %param.16) | copy-start | bytes 3145732
  72.4 60.2 %copy-start.4 = (f32[1024]{0:T(1024)S(1)}, f32[1024]{0:T(1024)}, u32[]{:S(2)}) copy-start(f32[1024]{0:T(1024)} %param.20) | copy-start | bytes 12292
  73.8 121.7 %all-to-all-start.1 = ((bf16[1,512,16,64]{1,3,0,2:T(8,128)(2,1)}), bf16[1,512,16,64]{1,3,0,2:T(8,128)(2,1)S(1)}, u32[]{:S(2)}, u32[]{:S(2)}) async-start(bf16[1,512,16,64]{1,3,0,2:T(8,128)(2,1)} %bitcast.6), calls=%async_computation.1 | async-start | bytes 2097152 | tf_op jit(solution)/shard_map/all_to_all | solution.py:153
  78.1 345.3 %all-gather.17.cloned.1.call-start = ((), (), s32[]{:S(2)}) async-start(), calls=%async_computation.12 | async-start | bytes 4325376 | tf_op jit(solution)/shard_map/all_gather | solution.py:140
  80.8 109.9 %copy-start.5 = (f32[1024]{0:T(1024)S(1)}, f32[1024]{0:T(1024)}, u32[]{:S(2)}) copy-start(f32[1024]{0:T(1024)} %param.19) | copy-start | bytes 12292
  195.5 32.8 %all-to-all-start = ((bf16[1,512,16,64]{1,3,0,2:T(8,128)(2,1)}), bf16[1,512,16,64]{1,3,0,2:T(8,128)(2,1)S(1)}, u32[]{:S(2)}, u32[]{:S(2)}) async-start(bf16[1,512,16,64]{1,3,0,2:T(8,128)(2,1)} %bitcast.2), calls=%async_computation | async-start | bytes 2097152 | tf_op jit(solution)/shard_map/all_to_all | solution.py:154
  219.8 8.5 %copy-start.2 = (bf16[4096,2,64]{0,2,1:T(8,128)(2,1)}, bf16[4096,2,64]{0,2,1:T(8,128)(2,1)S(1)}, u32[]{:S(2)}) copy-start(bf16[4096,2,64]{0,2,1:T(8,128)(2,1)S(1)} %get-tuple-element.491) | copy-start | bytes 3145732
  230.2 46.0 %copy-start.3 = (f32[2,1024]{1,0:T(2,128)S(1)}, f32[2,1024]{1,0:T(2,128)}, u32[]{:S(2)}) copy-start(f32[2,1024]{1,0:T(2,128)} %param.21) | copy-start | bytes 24580
  272.7 12.6 %all-to-all-start.2 = ((bf16[8,2,8192]{2,1,0:T(2,128)(2,1)}), bf16[8,2,8192]{2,1,0:T(2,128)(2,1)S(1)}, u32[]{:S(2)}, u32[]{:S(2)}) async-start(bf16[8,2,8192]{2,1,0:T(2,128)(2,1)} %reshape.311), calls=%async_computation.2 | async-start | bytes 524288 | tf_op jit(solution)/shard_map/all_to_all | solution.py:166
  357.6 27.3 %all-to-all-start.3 = ((bf16[1,128,3,16,64]{1,4,2,0,3:T(8,128)(2,1)}), bf16[1,128,3,16,64]{1,4,2,0,3:T(8,128)(2,1)S(1)}, u32[]{:S(2)}, u32[]{:S(2)}) async-start(bf16[1,128,3,16,64]{1,4,2,0,3:T(8,128)(2,1)} %copy.56), calls=%async_computation.3 | async-start | bytes 1572864 | tf_op jit(solution)/shard_map/all_to_all | solution.py:177
  399.9 23.5 %all-to-all-start.4 = ((bf16[8,1,128,2,64]{2,4,3,1,0:T(8,128)(2,1)}), bf16[8,1,128,2,64]{2,4,3,1,0:T(8,128)(2,1)S(1)}, u32[]{:S(2)}, u32[]{:S(2)}) async-start(bf16[8,1,128,2,64]{2,4,3,1,0:T(8,128)(2,1)} %constant_dynamic-update-slice_fusion), calls=%async_computation.4 | async-start | bytes 524288 | tf_op jit(solution)/shard_map/all_to_all | solution.py:14
  460.7 15.7 %copy-start = (bf16[2,1024,1024]{2,1,0:T(8,128)(2,1)S(1)}, bf16[2,1024,1024]{2,1,0:T(8,128)(2,1)}, u32[]{:S(2)}) copy-start(bf16[2,1024,1024]{2,1,0:T(8,128)(2,1)} %all-gather.17.cloned.1.call-done) | copy-start | bytes 12582916
Sparse Core Ops, SparseCore 0:
  10.2 58.9 all-gather.8
  72.0 60.5 all-gather.6
  135.5 55.0 all-gather.10
  193.4 61.0 all-gather.12
  257.3 95.1 all-gather.14
  355.3 68.0 all-gather.16
